TPU v7x, 32 devices: a whole 2x2x4 slice. The times are simulated.
32 devices in a mesh: shard: 2 (over core), ctx: 8 (over z, x), tp: 2 (over y).
Axes of the slice: x: 2, y: 2, z: 4, core: 2. Of those that a mesh axis runs over, the one named last changes fastest.
Arguments:
- tokens: bfloat16 [2, 4096, 1024], P('shard', ('ctx', 'tp')), may hold values from -6 to 6
- value_first: bfloat16 [2, 4096, 1024], P('shard', ('ctx', 'tp')), may hold values from -6 to 6
- teacher: bfloat16 [2, 4096, 1024], P('shard', ('ctx', 'tp')), may hold values from -13 to 13
- valid: int32 [2, 4096], P('shard', ('ctx', 'tp')), may hold values from 0 to 1, as said below
- blocks: int32 [2, 4096], P('shard'), may hold values from 0 to 31, never falling along the last dimension, each value on 1 to 256 neighbouring positions
- gain_attn: float32 [1024], replicated, may hold values from 0.1 to 1.9
- gain_ffn: float32 [1024], replicated, may hold values from 0.1 to 1.9
- w_query: bfloat16 [1024, 1024], P('shard', 'tp'), may hold values from -0.375 to 0.375
- w_key: bfloat16 [1024, 1024], P('shard', 'tp'), may hold values from -0.1875 to 0.1875
- w_value: bfloat16 [1024, 1024], P('shard', 'tp'), may hold values from -0.1875 to 0.1875
- w_out: bfloat16 [1024, 1024], P('tp', 'shard'), may hold values from -0.75 to 0.75
- w_gate: bfloat16 [1024, 2816], P('shard', 'tp'), may hold values from -0.1875 to 0.1875
- w_up: bfloat16 [1024, 2816], P('shard', 'tp'), may hold values from -0.1875 to 0.1875
- w_down: bfloat16 [2816, 1024], P('tp', 'shard'), may hold values from -0.109375 to 0.109375
Outputs:
- output: bfloat16 [2, 4096, 1024], P('shard', ('ctx', 'tp'))
- loss: float32 [], replicated
- tokens_grad: float32 [2, 4096, 1024], P('shard', ('ctx', 'tp'))
- value_first_grad: float32 [2, 4096, 1024], P('shard', ('ctx', 'tp'))
- gain_attn_grad: float32 [1024], replicated
- gain_ffn_grad: float32 [1024], replicated
- w_query_grad: float32 [1024, 1024], P('shard', 'tp')
- w_key_grad: float32 [1024, 1024], P('shard', 'tp')
- w_value_grad: float32 [1024, 1024], P('shard', 'tp')
- w_out_grad: float32 [1024, 1024], P('tp', 'shard')
- w_gate_grad: float32 [1024, 2816], P('shard', 'tp')
- w_up_grad: float32 [1024, 2816], P('shard', 'tp')
- w_down_grad: float32 [2816, 1024], P('tp', 'shard')
Inputs may be any that keep to these rules, and one draw needn't show every extreme that they name: `blocks`: block numbers count from 0 and never fall along a sequence; each block holds 1 to 256 tokens, one exactly 256. The first token of every sequence is valid.
All inputs are finite; a program needn't handle non-finite values.
Results may differ from a plain program's by a relative error of at most 0.019.
Values may be sent and summed in bfloat16 or wider, within the bound.
No kernel may reach another device: no remote copies, remote signals or barrier semaphores. Data moves between devices by JAX's collectives and lax.ppermute only.
A program may use at most 256 MiB of HBM per device.

v0:
```python
import jax
import jax.numpy as jnp
from jax import lax
from jax.sharding import PartitionSpec as P

HEAD_DIM = 64
epsilon = 1e-06


def rms_norm(values, gain):
    return values * lax.rsqrt(jnp.mean(values * values, axis=-1, keepdims=True) + epsilon) * gain


def product(left, right):
    return jnp.dot(left, right, preferred_element_type=jnp.float32)


def product_nt(left, right):
    return lax.dot_general(
        left, right, (((1,), (1,)), ((), ())), preferred_element_type=jnp.float32
    )


def product_tn(left, right):
    return lax.dot_general(
        left, right, (((0,), (0,)), ((), ())), preferred_element_type=jnp.float32
    )


def head_slice(values, head_index):
    return lax.dynamic_slice_in_dim(values, head_index * HEAD_DIM, HEAD_DIM, 1)


def block_layout(query_count):
    return (query_count, query_count // query_count)


def heads_to_columns(stacked):
    return jnp.transpose(stacked, (1, 0, 2)).reshape(
        stacked.shape[1], stacked.shape[0] * stacked.shape[2]
    )


def attend_forward(queries, keys_all, values_all, query_marks, key_marks):
    query_count = queries.shape[0]
    block_size, block_count = block_layout(query_count)
    score_scale = HEAD_DIM ** (-0.5)

    def one_head(head_index):
        query_head = head_slice(queries, head_index)
        key_head = head_slice(keys_all, head_index)
        value_head = head_slice(values_all, head_index)

        def one_block(block_index):
            scores = product_nt(query_head, key_head) * score_scale
            scores = jnp.where(key_marks[None, :] <= query_marks[:, None], scores, -1e30)
            highest = jnp.max(scores, axis=1, keepdims=True)
            exponent = jnp.exp(scores - highest)
            totals = jnp.sum(exponent, axis=1, keepdims=True)
            weights = (exponent / totals).astype(jnp.bfloat16)
            return (product(weights, value_head), (highest + jnp.log(totals))[:, 0])

        outputs, log_totals = lax.map(one_block, jnp.arange(block_count))
        return (outputs.reshape(query_count, HEAD_DIM), log_totals.reshape(query_count))

    outputs, log_totals = lax.map(one_head, jnp.arange(queries.shape[1] // HEAD_DIM))
    return (heads_to_columns(outputs), log_totals)


def attend_backward(
    queries, keys_all, values_all, grad_attended, log_totals, query_marks, key_marks
):
    query_count = queries.shape[0]
    block_size, block_count = block_layout(query_count)
    score_scale = HEAD_DIM ** (-0.5)

    def one_head(item):
        head_index, head_totals = item
        query_head = head_slice(queries, head_index)
        key_head = head_slice(keys_all, head_index)
        value_head = head_slice(values_all, head_index)
        grad_head = head_slice(grad_attended, head_index)

        def one_block(carry, block_index):
            scores = product_nt(query_head, key_head) * score_scale
            scores = jnp.where(key_marks[None, :] <= query_marks[:, None], scores, -1e30)
            probs = jnp.exp(scores - head_totals[:, None])
            grad_probs = product_nt(grad_head, value_head)
            inner = jnp.sum(probs * grad_probs, axis=1, keepdims=True)
            grad_scores = (probs * (grad_probs - inner)).astype(jnp.bfloat16)
            query_grad = product(grad_scores, key_head) * score_scale
            key_grad, value_grad = carry
            key_grad = key_grad + product_tn(grad_scores, query_head) * score_scale
            value_grad = value_grad + product_tn(probs.astype(jnp.bfloat16), grad_head)
            return ((key_grad, value_grad), (query_grad, inner[:, 0]))

        empty = jnp.zeros((keys_all.shape[0], HEAD_DIM), jnp.float32)
        start_carry = (empty, empty)
        sums, outs = lax.scan(one_block, start_carry, jnp.arange(block_count))
        query_grad = outs[0].reshape(query_count, HEAD_DIM)
        return (query_grad, sums[0], sums[1])

    head_count = queries.shape[1] // HEAD_DIM
    results = lax.map(one_head, (jnp.arange(head_count), log_totals))
    return (
        heads_to_columns(results[0]),
        heads_to_columns(results[1]),
        heads_to_columns(results[2]),
    )


def on_device(
    tokens,
    value_first,
    teacher,
    valid,
    blocks,
    gain_attn,
    gain_ffn,
    w_query,
    w_key,
    w_value,
    w_out,
    w_gate,
    w_up,
    w_down,
):
    width = tokens.shape[2]
    own_rows = tokens.shape[1]
    group_rows = own_rows * lax.axis_size("tp")
    inputs = tokens.reshape(own_rows, width).astype(jnp.float32)
    key_marks = blocks.reshape(-1)
    query_marks = lax.dynamic_slice_in_dim(
        key_marks, lax.axis_index("ctx") * group_rows, group_rows, 0
    )
    gathered = (
        lax.all_gather(w_query, "shard", axis=0, tiled=True),
        lax.all_gather(w_key, "shard", axis=0, tiled=True),
        lax.all_gather(w_value, "shard", axis=0, tiled=True),
        lax.all_gather(w_gate, "shard", axis=0, tiled=True),
        lax.all_gather(w_up, "shard", axis=0, tiled=True),
        lax.all_gather(w_out, "shard", axis=1, tiled=True),
        lax.all_gather(w_down, "shard", axis=1, tiled=True),
    )
    weight_query, weight_key, weight_value, weight_gate, weight_up, weight_out, weight_down = (
        gathered
    )

    def spread(values):
        return lax.all_gather(values, "tp", axis=0, tiled=True)

    def collect(terms):
        return lax.psum_scatter(terms, "tp", scatter_dimension=0, tiled=True)

    normed_one = spread(rms_norm(inputs, gain_attn).astype(jnp.bfloat16))
    first_mine = lax.all_to_all(
        value_first.reshape(own_rows, width), "tp", split_axis=1, concat_axis=0, tiled=True
    )
    queries = product(normed_one, weight_query).astype(jnp.bfloat16)
    keys = product(normed_one, weight_key).astype(jnp.bfloat16)
    mixed = (0.5 * product(normed_one, weight_value) + 0.5 * first_mine.astype(jnp.float32)).astype(
        jnp.bfloat16
    )
    keys_all, mixed_all = (
        lax.all_gather(keys, "ctx", axis=0, tiled=True),
        lax.all_gather(mixed, "ctx", axis=0, tiled=True),
    )
    attended, log_totals = attend_forward(queries, keys_all, mixed_all, query_marks, key_marks)
    attended = attended.astype(jnp.bfloat16)
    hidden = inputs + collect(product(attended, weight_out))
    normed_two = spread(rms_norm(hidden, gain_ffn).astype(jnp.bfloat16))
    gate_value = product(normed_two, weight_gate)
    up_value = product(normed_two, weight_up)
    logistic = jax.nn.sigmoid(gate_value)
    activated = (gate_value * logistic * up_value).astype(jnp.bfloat16)
    final = hidden + collect(product(activated, weight_down))
    target = teacher.reshape(own_rows, width).astype(jnp.float32)
    keep = valid.reshape(own_rows).astype(jnp.float32)
    difference = final - target
    local_error = jnp.sum(jnp.mean(difference * difference, axis=1) * keep)
    error_sum, valid_count = lax.psum((local_error, jnp.sum(keep)), ("shard", "ctx", "tp"))
    loss = error_sum / valid_count
    token_total = group_rows * lax.axis_size("ctx") * lax.axis_size("shard")
    grad_final = token_total / valid_count * keep[:, None] * difference
    grad_round = spread(grad_final.astype(jnp.bfloat16))
    grad_act = product_nt(grad_round, weight_down)
    grad_gate = (grad_act * up_value * logistic * (1.0 + gate_value * (1.0 - logistic))).astype(
        jnp.bfloat16
    )
    grad_up = (grad_act * gate_value * logistic).astype(jnp.bfloat16)
    grad_two = collect(product_nt(grad_gate, weight_gate) + product_nt(grad_up, weight_up))
    norm_two_back = jax.vjp(rms_norm, hidden, gain_ffn)[1]
    hidden_part, gain_ffn_term = norm_two_back(grad_two)
    grad_hidden = grad_final + hidden_part
    hidden_round = spread(grad_hidden.astype(jnp.bfloat16))
    grad_attended = product_nt(hidden_round, weight_out).astype(jnp.bfloat16)
    query_grad, key_term, value_term = attend_backward(
        queries, keys_all, mixed_all, grad_attended, log_totals, query_marks, key_marks
    )
    key_sum, value_sum = (
        lax.psum_scatter(
            key_term.astype(jnp.bfloat16), "ctx", scatter_dimension=0, tiled=True
        ).astype(jnp.float32),
        lax.psum_scatter(
            value_term.astype(jnp.bfloat16), "ctx", scatter_dimension=0, tiled=True
        ).astype(jnp.float32),
    )
    query_round = query_grad.astype(jnp.bfloat16)
    key_round = key_sum.astype(jnp.bfloat16)
    value_half = (0.5 * value_sum).astype(jnp.bfloat16)
    grad_one = collect(
        product_nt(query_round, weight_query)
        + product_nt(key_round, weight_key)
        + product_nt(value_half, weight_value)
    )
    norm_one_back = jax.vjp(rms_norm, inputs, gain_attn)[1]
    input_part, gain_attn_term = norm_one_back(grad_one)
    tokens_grad = grad_hidden + input_part
    first_grad = lax.all_to_all(value_half, "tp", split_axis=0, concat_axis=1, tiled=True).astype(
        jnp.float32
    )
    gain_attn_grad, gain_ffn_grad = lax.psum(
        (gain_attn_term, gain_ffn_term), ("shard", "ctx", "tp")
    )
    piece = lax.psum_scatter(
        jnp.concatenate(
            [
                product_tn(normed_one, query_round),
                product_tn(normed_one, key_round),
                product_tn(normed_one, value_half),
                product_tn(hidden_round, attended),
                product_tn(normed_two, grad_gate),
                product_tn(normed_two, grad_up),
                product_tn(grad_round, activated),
            ],
            axis=1,
        ).astype(jnp.bfloat16),
        "shard",
        scatter_dimension=0,
        tiled=True,
    )
    summed = lax.psum(piece, "ctx").astype(jnp.float32)
    half_width = w_query.shape[1]
    hidden_width = w_gate.shape[1]
    offset_gate = 4 * half_width
    offset_up = offset_gate + hidden_width
    offset_down = offset_up + hidden_width
    w_query_grad = summed[:, 0:half_width]
    w_key_grad = summed[:, half_width : 2 * half_width]
    w_value_grad = summed[:, 2 * half_width : 3 * half_width]
    w_out_grad = jnp.transpose(summed[:, 3 * half_width : offset_gate])
    w_gate_grad = summed[:, offset_gate:offset_up]
    w_up_grad = summed[:, offset_up:offset_down]
    w_down_grad = jnp.transpose(summed[:, offset_down : offset_down + hidden_width])
    output = final.astype(jnp.bfloat16).reshape(1, own_rows, width)
    return (
        output,
        loss,
        tokens_grad.reshape(1, own_rows, width),
        first_grad.reshape(1, own_rows, width),
        gain_attn_grad,
        gain_ffn_grad,
        w_query_grad,
        w_key_grad,
        w_value_grad,
        w_out_grad,
        w_gate_grad,
        w_up_grad,
        w_down_grad,
    )


def solution(mesh):
    placed = (
        P("shard", ("ctx", "tp"), None),
        P("shard", ("ctx", "tp"), None),
        P("shard", ("ctx", "tp"), None),
        P("shard", ("ctx", "tp")),
        P("shard", None),
        P(),
        P(),
        P("shard", "tp"),
        P("shard", "tp"),
        P("shard", "tp"),
        P("tp", "shard"),
        P("shard", "tp"),
        P("shard", "tp"),
        P("tp", "shard"),
    )
    return jax.shard_map(
        on_device,
        mesh=mesh,
        in_specs=placed,
        out_specs=(
            P("shard", ("ctx", "tp"), None),
            P(),
            P("shard", ("ctx", "tp"), None),
            P("shard", ("ctx", "tp"), None),
            P(),
            P(),
            P("shard", "tp"),
            P("shard", "tp"),
            P("shard", "tp"),
            P("tp", "shard"),
            P("shard", "tp"),
            P("shard", "tp"),
            P("tp", "shard"),
        ),
        check_vma=False,
    )
```

profile of v0, /device:TPU:0, one launch (start us, length us, event | category | flops | bytes accessed | tf_op | source)
XLA Modules:
  0.0 1274.1 jit_solution(9744088578391808102)
XLA Ops:
  13.7 7.6 all-gather.18.cloned.1.call-done
  21.3 24.6 %all-gather.14.cloned.1.call-done = bf16[512,1024]{1,0:T(8,128)(2,1)} async-done(((bf16[256,1024]{1,0:T(8,128)(2,1)}), bf16[512,1024]{1,0:T(8,128)(2,1)}) %all-gather.14.cloned.1.call-update) | async-done | bytes 1048592 | tf_op jit(solution)/shard_map/all_gather | solution.py:150
  49.5 10.7 all_to_all.26
  70.1 75.2 %all-gather.20.cloned.1.call-done = bf16[4096,512]{1,0:T(8,128)(2,1)} async-done(((bf16[512,512]{1,0:T(8,128)(2,1)}), bf16[4096,512]{1,0:T(8,128)(2,1)}) %all-gather.20.cloned.1.call-update) | async-done | bytes 4194320 | tf_op jit(solution)/shard_map/all_gather | solution.py:165
  145.3 74.2 %all-gather.24.cloned.1.call-done = bf16[4096,512]{1,0:T(8,128)(2,1)} async-done(((bf16[512,512]{1,0:T(8,128)(2,1)}), bf16[4096,512]{1,0:T(8,128)(2,1)}) %all-gather.24.cloned.1.call-update) | async-done | bytes 4194320 | tf_op jit(solution)/shard_map/all_gather | solution.py:166
  219.6 73.0 %while.10 = (s32[]{:T(128)}, bf16[8,512,64]{1,2,0:T(8,128)(2,1)S(1)}, f32[8,512]{1,0:T(8,128)S(1)}, s32[1,4096]{1,0:T(1,128)S(1)}, s32[512]{0:T(512)S(1)}, /*ind...) while((s32[]{:T(128)}, ...), condition=%wide.region_4.0_spmd, body=%wide.region_1.4_spmd.sunk | while | flops 555744768 | bytes 27565260 | solution.py:66
  297.0 29.4 %reduce-scatter.8.cloned.1.call-done = f32[256,1024]{1,0:T(8,128)} async-done(((f32[512,1024]{1,0:T(8,128)}), f32[256,1024]{1,0:T(8,128)}) %reduce-scatter.8.cloned.1.call-update) | async-done | bytes 1048592 | tf_op jit(solution)/shard_map/reduce_scatter | solution.py:153
  330.4 9.4 all-gather.30.cloned.1.call-done
  339.8 24.6 %all-gather.28.cloned.1.call-done = bf16[512,1024]{1,0:T(8,128)(2,1)} async-done(((bf16[256,1024]{1,0:T(8,128)(2,1)}), bf16[512,1024]{1,0:T(8,128)(2,1)}) %all-gather.28.cloned.1.call-update) | async-done | bytes 1048592 | tf_op jit(solution)/shard_map/all_gather | solution.py:150
  370.0 7.8 all-gather.32.cloned.1.call-done
  384.4 7.8 all-gather.34.cloned.1.call-done
  398.3 40.9 %psum.36 = f32[]{:T(128)} all-reduce(f32[]{:T(128)} %convert_reduce_fusion), channel_id=1, replica_groups=mesh['shard'=2,'ctx'=8,'tp'=2] {'shard','ctx','tp'}, use_global_device_ids=true, to_apply=%region_12.13 | all-reduce | flops 1 | bytes 8 | tf_op jit(solution)/shard_map/psum | solution.py:181
  442.2 21.4 %all-gather.36.cloned.1.call-done = bf16[512,1024]{1,0:T(8,128)(2,1)} async-done(((bf16[256,1024]{1,0:T(8,128)(2,1)}), bf16[512,1024]{1,0:T(8,128)(2,1)}) %all-gather.36.cloned.1.call-update) | async-done | bytes 1048592 | tf_op jit(solution)/shard_map/all_gather | solution.py:150
  476.2 31.9 %reduce-scatter.12.cloned.1.call-done = f32[256,1024]{1,0:T(8,128)} async-done(((f32[512,1024]{1,0:T(8,128)}), f32[256,1024]{1,0:T(8,128)}) %reduce-scatter.12.cloned.1.call-update) | async-done | bytes 1048592 | tf_op jit(solution)/shard_map/reduce_scatter | solution.py:153
  512.6 21.2 %all-gather.38.cloned.1.call-done = bf16[512,1024]{1,0:T(8,128)(2,1)} async-done(((bf16[256,1024]{1,0:T(8,128)(2,1)}), bf16[512,1024]{1,0:T(8,128)(2,1)}) %all-gather.38.cloned.1.call-update) | async-done | bytes 1048592 | tf_op jit(solution)/shard_map/all_gather | solution.py:150
  536.1 233.1 %while.27 = (s32[]{:T(128)}, bf16[8,512,64]{1,2,0:T(8,128)(2,1)S(1)}, bf16[8,4096,64]{1,2,0:T(8,128)(2,1)}, bf16[8,4096,64]{1,2,0:T(8,128)(2,1)}, s32[1,4096]{1,...) while((s32[]{:T(128)}, ...), condition=%wide.region_17.18_spmd, body=%wide.region_15.17_spmd.sunk | while | flops 1363443200 | bytes 102398224 | solution.py:104
  547.4 7.9 multiply_convert_fusion.10
  576.5 7.9 multiply_convert_fusion.10
  598.2 7.5 multiply_reduce_fusion.7
  605.6 7.9 multiply_convert_fusion.10
  634.8 7.9 multiply_convert_fusion.10
  663.9 7.9 multiply_convert_fusion.10
  693.0 7.9 multiply_convert_fusion.10
  722.2 7.9 multiply_convert_fusion.10
  751.3 7.9 multiply_convert_fusion.10
  783.2 74.6 %reduce-scatter.14.cloned.1.call-done = bf16[512,512]{0,1:T(8,128)(2,1)} async-done(((bf16[4096,512]{0,1:T(8,128)(2,1)}), bf16[512,512]{0,1:T(8,128)(2,1)}) %reduce-scatter.14.cloned.1.call-update) | async-done | bytes 524304 | tf_op jit(solution)/shard_map/reduce_scatter | solution.py:201
  860.5 88.7 %reduce-scatter.16.cloned.1.call-done = bf16[512,512]{1,0:T(8,128)(2,1)} async-done(((bf16[4096,512]{1,0:T(8,128)(2,1)}), bf16[512,512]{1,0:T(8,128)(2,1)}) %reduce-scatter.16.cloned.1.call-update) | async-done | bytes 524304 | tf_op jit(solution)/shard_map/reduce_scatter | solution.py:204
  973.8 15.7 %reduce-scatter.20.cloned.1.call-done = bf16[512,6272]{1,0:T(8,128)(2,1)} async-done(((bf16[1024,6272]{1,0:T(8,128)(2,1)}), bf16[512,6272]{1,0:T(8,128)(2,1)}) %reduce-scatter.20.cloned.1.call-update) | async-done | bytes 6422544 | tf_op jit(solution)/shard_map/reduce_scatter | solution.py:225
  994.7 10.0 all-to-all-done.1
  1007.4 19.2 %reduce-scatter.18.cloned.1.call-done = f32[256,1024]{1,0:T(8,128)} async-done(((f32[512,1024]{1,0:T(8,128)}), f32[256,1024]{1,0:T(8,128)}) %reduce-scatter.18.cloned.1.call-update) | async-done | bytes 1048592 | tf_op jit(solution)/shard_map/reduce_scatter | solution.py:153
  1028.2 43.5 %all-reduce = (f32[]{:T(128)}, f32[1024]{0:T(1024)}, f32[1024]{0:T(1024)}) all-reduce(f32[]{:T(128)} %multiply_reduce_fusion.5, f32[1024]{0:T(1024)S(1)} %get-tuple-element.215, f32[1024]{0:T(1024)S(1)} %copy-done.19), channel_id=1, replica_groups=mesh['shard'=2,'ctx'=8,'tp'=2] {'shard','ctx','tp'}, use_global_device_ids=true, to_apply=%region_10.11 | all-reduce | flops 2049 | bytes 16392 | tf_op jit(solution)/shard_map/psum | solution.py:181
  1075.7 172.6 %all-reduce.3.cloned.1.call-done = bf16[512,6272]{1,0:T(8,128)(2,1)} async-done(((bf16[512,6272]{1,0:T(8,128)(2,1)}), bf16[512,6272]{1,0:T(8,128)(2,1)}) %all-reduce.3.cloned.1.call-update) | async-done | bytes 6422544 | tf_op jit(solution)/shard_map/psum | solution.py:242
  (309 shorter events, 362.9 us)
Async XLA Ops:
  7.2 14.1 %all-gather.18.cloned.1.call-start = ((), (), s32[]{:S(2)}) async-start(), calls=%async_computation.11 | async-start | bytes 1572864 | tf_op jit(solution)/shard_map/all_gather | solution.py:138
  7.9 38.0 %all-gather.14.cloned.1.call-start = ((), (), s32[]{:S(2)}) async-start(), calls=%async_computation.9 | async-start | bytes 1572864 | tf_op jit(solution)/shard_map/all_gather | solution.py:150
  12.4 36.7 %copy-start.15 = (bf16[1,256,1024]{2,1,0:T(8,128)(2,1)S(1)}, bf16[1,256,1024]{2,1,0:T(8,128)(2,1)}, u32[]{:S(2)}) copy-start(bf16[1,256,1024]{2,1,0:T(8,128)(2,1)} %param.19) | copy-start | bytes 1572868
  12.4 48.0 %all-gather.22.cloned.1.call-start = ((), (), s32[]{:S(2)}) async-start(), calls=%async_computation.13 | async-start | bytes 1572864 | tf_op jit(solution)/shard_map/all_gather | solution.py:139
  13.1 55.1 %all-gather.16.cloned.1.call-start = ((), (), s32[]{:S(2)}) async-start(), calls=%async_computation.10 | async-start | bytes 1572864 | tf_op jit(solution)/shard_map/all_gather | solution.py:137
  13.7 131.6 %all-gather.20.cloned.1.call-start = ((), (), s32[]{:S(2)}) async-start(), calls=%async_computation.12 | async-start | bytes 4718592 | tf_op jit(solution)/shard_map/all_gather | solution.py:165
  49.0 170.6 %all-gather.24.cloned.1.call-start = ((), (), s32[]{:S(2)}) async-start(), calls=%async_computation.14 | async-start | bytes 4718592 | tf_op jit(solution)/shard_map/all_gather | solution.py:166
  63.1 229.6 %all-gather.26.cloned.1.call-start = ((), (), s32[]{:S(2)}) async-start(), calls=%async_computation.15 | async-start | bytes 1572864 | tf_op jit(solution)/shard_map/all_gather | solution.py:142
  63.9 262.6 %reduce-scatter.8.cloned.1.call-start = ((), (), s32[]{:S(2)}) async-start(), calls=%async_computation.16 | async-start | bytes 3145728 | tf_op jit(solution)/shard_map/reduce_scatter | solution.py:153
  292.7 33.7 %copy-start.1 = (bf16[1,256,1024]{2,1,0:T(8,128)(2,1)S(1)}, bf16[1,256,1024]{2,1,0:T(8,128)(2,1)}, u32[]{:S(2)}) copy-start(bf16[1,256,1024]{2,1,0:T(8,128)(2,1)} %param.18) | copy-start | bytes 1572868
  296.2 31.7 %copy-start.17 = (f32[1024]{0:T(1024)S(1)}, f32[1024]{0:T(1024)}, u32[]{:S(2)}) copy-start(f32[1024]{0:T(1024)} %param.24) | copy-start | bytes 12292
  296.2 43.6 %all-gather.30.cloned.1.call-start = ((), (), s32[]{:S(2)}) async-start(), calls=%async_computation.18 | async-start | bytes 4325376 | tf_op jit(solution)/shard_map/all_gather | solution.py:140
  297.0 67.4 %all-gather.28.cloned.1.call-start = ((), (), s32[]{:S(2)}) async-start(), calls=%async_computation.17 | async-start | bytes 1572864 | tf_op jit(solution)/shard_map/all_gather | solution.py:150
  328.9 48.9 %all-gather.32.cloned.1.call-start = ((), (), s32[]{:S(2)}) async-start(), calls=%async_computation.19 | async-start | bytes 4325376 | tf_op jit(solution)/shard_map/all_gather | solution.py:141
  329.6 62.6 %all-gather.34.cloned.1.call-start = ((), (), s32[]{:S(2)}) async-start(), calls=%async_computation.20 | async-start | bytes 4325376 | tf_op jit(solution)/shard_map/all_gather | solution.py:143
  330.2 109.7 %reduce-scatter.10.cloned.1.call-start = ((), (), s32[]{:S(2)}) async-start(), calls=%async_computation.21 | async-start | bytes 3145728 | tf_op jit(solution)/shard_map/reduce_scatter | solution.py:153
  392.2 47.7 %copy-start.4 = (bf16[1,256,1024]{2,1,0:T(8,128)(2,1)S(1)}, bf16[1,256,1024]{2,1,0:T(8,128)(2,1)}, u32[]{:S(2)}) copy-start(bf16[1,256,1024]{2,1,0:T(8,128)(2,1)} %param.20) | copy-start | bytes 1572868
  397.6 66.0 %all-gather.36.cloned.1.call-start = ((), (), s32[]{:S(2)}) async-start(), calls=%async_computation.22 | async-start | bytes 1572864 | tf_op jit(solution)/shard_map/all_gather | solution.py:150
  442.1 66.0 %reduce-scatter.12.cloned.1.call-start = ((), (), s32[]{:S(2)}) async-start(), calls=%async_computation.23 | async-start | bytes 3145728 | tf_op jit(solution)/shard_map/reduce_scatter | solution.py:153
  473.0 35.2 %copy-start.3 = (f32[256,1024]{1,0:T(8,128)S(1)}, f32[256,1024]{1,0:T(8,128)}, u32[]{:S(2)}) copy-start(f32[256,1024]{1,0:T(8,128)} %reduce-scatter.10.cloned.1.call-done) | copy-start | bytes 3145732
  476.2 57.6 %all-gather.38.cloned.1.call-start = ((), (), s32[]{:S(2)}) async-start(), calls=%async_computation.24 | async-start | bytes 1572864 | tf_op jit(solution)/shard_map/all_gather | solution.py:150
  512.3 345.5 %reduce-scatter.14.cloned.1.call-start = ((), (), s32[]{:S(2)}) async-start(), calls=%async_computation.25 | async-start | bytes 4718592 | tf_op jit(solution)/shard_map/reduce_scatter | solution.py:201
  769.2 180.0 %reduce-scatter.16.cloned.1.call-start = ((), (), s32[]{:S(2)}) async-start(), calls=%async_computation.26 | async-start | bytes 4718592 | tf_op jit(solution)/shard_map/reduce_scatter | solution.py:204
  775.9 213.6 %reduce-scatter.20.cloned.1.call-start = ((), (), s32[]{:S(2)}) async-start(), calls=%async_computation.28 | async-start | bytes 19267584 | tf_op jit(solution)/shard_map/reduce_scatter | solution.py:225
  967.8 58.8 %reduce-scatter.18.cloned.1.call-start = ((), (), s32[]{:S(2)}) async-start(), calls=%async_computation.27 | async-start | bytes 3145728 | tf_op jit(solution)/shard_map/reduce_scatter | solution.py:153
  973.7 274.6 %all-reduce.3.cloned.1.call-start = ((), (), s32[]{:S(2)}) async-start(), calls=%async_computation.29 | async-start | bytes 12845056 | tf_op jit(solution)/shard_map/psum | solution.py:242
  990.4 14.2 %all-to-all-start.1 = ((bf16[2,256,512]{2,1,0:T(8,128)(2,1)}), bf16[2,256,512]{2,1,0:T(8,128)(2,1)S(1)}, u32[]{:S(2)}, u32[]{:S(2)}) async-start(bf16[2,256,512]{2,1,0:T(8,128)(2,1)} %bitcast.27), calls=%async_computation.7 | async-start | bytes 1048576 | tf_op jit(solution)/shard_map/all_to_all | solution.py:219
  994.6 32.0 %copy-start.2 = (bf16[1,256,1024]{2,1,0:T(8,128)(2,1)S(1)}, bf16[1,256,1024]{2,1,0:T(8,128)(2,1)}, u32[]{:S(2)}) copy-start(bf16[1,256,1024]{2,1,0:T(8,128)(2,1)} %param.18) | copy-start | bytes 1572868
  994.6 32.0 %copy-start.18 = (f32[1024]{0:T(1024)S(1)}, f32[1024]{0:T(1024)}, u32[]{:S(2)}) copy-start(f32[1024]{0:T(1024)} %param.23) | copy-start | bytes 12292
  994.6 32.0 %copy-start.21 = (f32[256]{0:T(256)S(1)}, f32[256]{0:T(256)}, u32[]{:S(2)}) copy-start(f32[256]{0:T(256)} %copy-done.20) | copy-start | bytes 3076
  1004.7 68.3 %copy-start.23 = (f32[256]{0:T(256)S(1)}, f32[256]{0:T(256)}, u32[]{:S(2)}) copy-start(f32[256]{0:T(256)} %copy-done.22) | copy-start | bytes 3076
  1004.7 68.3 %copy-start.5 = (f32[256,1024]{1,0:T(8,128)S(1)}, f32[256,1024]{1,0:T(8,128)}, u32[]{:S(2)}) copy-start(f32[256,1024]{1,0:T(8,128)} %get-tuple-element.264) | copy-start | bytes 3145732
  (35 other events, 215.4 us)
Sparse Core Ops, SparseCore 0:
  9.6 11.7 all-gather.17
  23.4 22.4 all-gather.13
  47.5 9.0 all-gather.21
  58.0 10.1 all-gather.15
  70.8 74.5 all-gather.19
  147.9 71.6 all-gather.23
  221.1 7.2 all-gather.25
  296.3 30.0 reduce-scatter.7
  328.0 11.7 all-gather.29
  341.8 22.4 all-gather.27
  366.0 11.7 all-gather.31
  379.2 12.8 all-gather.33
  397.7 33.4 reduce-scatter.9
  442.3 21.2 all-gather.35
  476.3 31.8 reduce-scatter.11
  512.4 21.2 all-gather.37
  769.3 88.4 reduce-scatter.13
  861.3 87.7 reduce-scatter.15
  967.9 21.5 reduce-scatter.19
  992.2 34.3 reduce-scatter.17
  1030.4 217.8 all-reduce.2
where the time goes:
time: 1280 us; the launch traced here: 1270 us
  waiting for transfers between devices  725 us (57%)
  matrix products  278 us (22%)
  other arithmetic  95.9 us (7%)
  blocking collectives  95.1 us (7%)
  local copies, waits for them, and re-layouts  45.2 us (4%)
  between operations  18.3 us (1%)
    psum x1, waiting for transfers between devices, on_device(): summed = lax.psum(piece, 'ctx').astype(jnp.float32)  173 us
    dot_general x31, matrix products, product_nt(): lax.dot_general(left, right, (((1,), (1,)), ((), ())), preferred_element_...  123 us
    all_gather x4, waiting for transfers between devices, spread(): return lax.all_gather(values, 'tp', axis=0, tiled=True)  91.8 us
    reduce_scatter x1, waiting for transfers between devices, on_device(): lax.psum_scatter(value_term.astype(jnp.bfloat16), 'ctx', scatter_dimensio...  88.7 us
    psum x2, blocking collectives, on_device(): lax.psum((local_error, jnp.sum(keep)), ('shard', 'ctx', 'tp'))  84.4 us
    reduce_scatter x4, waiting for transfers between devices, collect(): return lax.psum_scatter(terms, 'tp', scatter_dimension=0, tiled=True)  80.5 us
    dot_general x23, matrix products, product(): return jnp.dot(left, right, preferred_element_type=jnp.float32)  79.6 us
    dot_general x23, matrix products, product_tn(): lax.dot_general(left, right, (((0,), (0,)), ((), ())), preferred_element_...  75.3 us
  transfers between devices with their start and end apart: 22, of which 19 were waited for; matrix products, arithmetic and copies ran while one was open for 10% of the time, Pallas kernels for 0%

commit v1 on v0

--- a/solution.py
+++ b/solution.py
@@ -1,3 +1,4 @@
+import functools
 import jax
 import jax.numpy as jnp
 from jax import lax
@@ -5,6 +6,14 @@
 
 HEAD_DIM = 64
 epsilon = 1e-06
+
+
+def track_lane(w_in, axis_name):
+    state_next = jnp.sum(lax.all_gather(w_in, axis_name), 0)
+    return state_next
+
+
+_bind_fields = functools.partial(track_lane, axis_name="ctx")
 
 
 def rms_norm(values, gain):
@@ -239,7 +248,7 @@
         scatter_dimension=0,
         tiled=True,
     )
-    summed = lax.psum(piece, "ctx").astype(jnp.float32)
+    summed = _bind_fields(piece).astype(jnp.float32)
     half_width = w_query.shape[1]
     hidden_width = w_gate.shape[1]
     offset_gate = 4 * half_width

time: 1280 us -> 2040 us (1.59)
  waiting for transfers between devices: 725 us -> 1400 us
  blocking collectives: 95.1 us -> 174 us
  other arithmetic: 95.9 us -> 123 us
  matrix products: 278 us -> 253 us
    all_gather x0 -> x1, waiting for transfers between devices: none -> 848 us  [track_lane(): state_next = jnp.sum(lax.all_gather(w_in, axis_name), 0)]
    psum x1 -> x0, waiting for transfers between devices: 173 us -> none  [on_device(): summed = lax.psum(piece, 'ctx').astype(jnp.float32)]
    psum x2, blocking collectives: 84.4 us -> 163 us  [on_device(): lax.psum((local_error, jnp.sum(keep)), ('shard', 'ctx', 'tp'))]
    dot_general x23, matrix products: 75.3 us -> 47.9 us  [product_tn(): lax.dot_general(left, right, (((0,), (0,)), ((), ())), preferred_element_...]
    reduce_sum x0 -> x1, other arithmetic: none -> 22 us  [track_lane(): state_next = jnp.sum(lax.all_gather(w_in, axis_name), 0)]
  transfers between devices with their start and end apart: 22 -> 22, of which waited for: 19 -> 19; matrix products, arithmetic and copies ran while one was open for 10% -> 6% of each run, Pallas kernels for 0% -> 0%
where the time goes in v1:
time: 2040 us; the launch traced here: 2030 us
  waiting for transfers between devices  1400 us (69%)
  matrix products  253 us (12%)
  blocking collectives  174 us (9%)
  other arithmetic  123 us (6%)
  local copies, waits for them, and re-layouts  45.8 us (2%)
    all_gather x1, waiting for transfers between devices, track_lane(): state_next = jnp.sum(lax.all_gather(w_in, axis_name), 0)  848 us
    psum x2, blocking collectives, on_device(): lax.psum((local_error, jnp.sum(keep)), ('shard', 'ctx', 'tp'))  163 us
    dot_general x31, matrix products, product_nt(): lax.dot_general(left, right, (((1,), (1,)), ((), ())), preferred_element_...  124 us
    all_gather x4, waiting for transfers between devices, spread(): return lax.all_gather(values, 'tp', axis=0, tiled=True)  89.2 us
    reduce_scatter x1, waiting for transfers between devices, on_device(): lax.psum_scatter(value_term.astype(jnp.bfloat16), 'ctx', scatter_dimensio...  88.7 us
    dot_general x23, matrix products, product(): return jnp.dot(left, right, preferred_element_type=jnp.float32)  80.9 us
    reduce_scatter x4, waiting for transfers between devices, collect(): return lax.psum_scatter(terms, 'tp', scatter_dimension=0, tiled=True)  80.4 us
    reduce_scatter x1, waiting for transfers between devices, on_device(): lax.psum_scatter(key_term.astype(jnp.bfloat16), 'ctx', scatter_dimension=...  75.3 us
  transfers between devices with their start and end apart: 22, of which 19 were waited for; matrix products, arithmetic and copies ran while one was open for 6% of the time, Pallas kernels for 0%

profile of v1, /device:TPU:0, one launch (start us, length us, event | category | flops | bytes accessed | tf_op | source)
XLA Modules:
  0.0 2031.4 jit_solution(12606343090748259480)
XLA Ops:
  13.8 22.1 %all-gather.16.cloned.1.call-done = bf16[512,1024]{1,0:T(8,128)(2,1)} async-done(((bf16[256,1024]{1,0:T(8,128)(2,1)}), bf16[512,1024]{1,0:T(8,128)(2,1)}) %all-gather.16.cloned.1.call-update) | async-done | bytes 1048592 | tf_op jit(solution)/shard_map/all_gather | solution.py:159
  35.9 10.6 all-gather.20.cloned.1.call-done
  50.1 11.2 all_to_all.26
  71.8 75.2 %all-gather.22.cloned.1.call-done = bf16[4096,512]{1,0:T(8,128)(2,1)} async-done(((bf16[512,512]{1,0:T(8,128)(2,1)}), bf16[4096,512]{1,0:T(8,128)(2,1)}) %all-gather.22.cloned.1.call-update) | async-done | bytes 4194320 | tf_op jit(solution)/shard_map/all_gather | solution.py:174
  147.1 74.2 %all-gather.26.cloned.1.call-done = bf16[4096,512]{1,0:T(8,128)(2,1)} async-done(((bf16[512,512]{1,0:T(8,128)(2,1)}), bf16[4096,512]{1,0:T(8,128)(2,1)}) %all-gather.26.cloned.1.call-update) | async-done | bytes 4194320 | tf_op jit(solution)/shard_map/all_gather | solution.py:175
  221.4 73.0 %while.10 = (s32[]{:T(128)}, bf16[8,512,64]{1,2,0:T(8,128)(2,1)S(1)}, f32[8,512]{1,0:T(8,128)S(1)}, s32[1,4096]{1,0:T(1,128)S(1)}, s32[512]{0:T(512)S(1)}, /*ind...) while((s32[]{:T(128)}, ...), condition=%wide.region_4.0_spmd, body=%wide.region_1.4_spmd.sunk | while | flops 555744768 | bytes 27565260 | solution.py:75
  298.7 29.4 %reduce-scatter.8.cloned.1.call-done = f32[256,1024]{1,0:T(8,128)} async-done(((f32[512,1024]{1,0:T(8,128)}), f32[256,1024]{1,0:T(8,128)}) %reduce-scatter.8.cloned.1.call-update) | async-done | bytes 1048592 | tf_op jit(solution)/shard_map/reduce_scatter | solution.py:162
  332.1 9.4 all-gather.32.cloned.1.call-done
  341.6 24.6 %all-gather.30.cloned.1.call-done = bf16[512,1024]{1,0:T(8,128)(2,1)} async-done(((bf16[256,1024]{1,0:T(8,128)(2,1)}), bf16[512,1024]{1,0:T(8,128)(2,1)}) %all-gather.30.cloned.1.call-update) | async-done | bytes 1048592 | tf_op jit(solution)/shard_map/all_gather | solution.py:159
  386.1 7.8 all-gather.36.cloned.1.call-done
  400.0 40.9 %psum.29 = f32[]{:T(128)} all-reduce(f32[]{:T(128)} %convert_reduce_fusion), channel_id=1, replica_groups=mesh['shard'=2,'ctx'=8,'tp'=2] {'shard','ctx','tp'}, use_global_device_ids=true, to_apply=%region_12.13 | all-reduce | flops 1 | bytes 8 | tf_op jit(solution)/shard_map/psum | solution.py:190
  443.9 21.4 %all-gather.38.cloned.1.call-done = bf16[512,1024]{1,0:T(8,128)(2,1)} async-done(((bf16[256,1024]{1,0:T(8,128)(2,1)}), bf16[512,1024]{1,0:T(8,128)(2,1)}) %all-gather.38.cloned.1.call-update) | async-done | bytes 1048592 | tf_op jit(solution)/shard_map/all_gather | solution.py:159
  477.9 31.9 %reduce-scatter.12.cloned.1.call-done = f32[256,1024]{1,0:T(8,128)} async-done(((f32[512,1024]{1,0:T(8,128)}), f32[256,1024]{1,0:T(8,128)}) %reduce-scatter.12.cloned.1.call-update) | async-done | bytes 1048592 | tf_op jit(solution)/shard_map/reduce_scatter | solution.py:162
  514.3 21.2 %all-gather.40.cloned.1.call-done = bf16[512,1024]{1,0:T(8,128)(2,1)} async-done(((bf16[256,1024]{1,0:T(8,128)(2,1)}), bf16[512,1024]{1,0:T(8,128)(2,1)}) %all-gather.40.cloned.1.call-update) | async-done | bytes 1048592 | tf_op jit(solution)/shard_map/all_gather | solution.py:159
  537.9 207.3 %while.27 = (s32[]{:T(128)}, bf16[8,512,64]{1,2,0:T(8,128)(2,1)S(1)}, bf16[8,4096,64]{1,2,0:T(8,128)(2,1)}, bf16[8,4096,64]{1,2,0:T(8,128)(2,1)}, s32[1,4096]{1,...) while((s32[]{:T(128)}, ...), condition=%wide.region_17.18_spmd, body=%wide.region_15.17_spmd.sunk | while | flops 1363443200 | bytes 135952688 | solution.py:113
  549.1 7.9 multiply_convert_fusion.10
  575.0 7.9 multiply_convert_fusion.10
  600.9 7.9 multiply_convert_fusion.10
  626.9 7.9 multiply_convert_fusion.10
  652.8 7.9 multiply_convert_fusion.10
  678.7 7.9 multiply_convert_fusion.10
  704.6 7.9 multiply_convert_fusion.10
  730.5 7.9 multiply_convert_fusion.10
  758.5 75.3 %reduce-scatter.14.cloned.1.call-done = bf16[512,512]{0,1:T(8,128)(2,1)} async-done(((bf16[4096,512]{0,1:T(8,128)(2,1)}), bf16[512,512]{0,1:T(8,128)(2,1)}) %reduce-scatter.14.cloned.1.call-update) | async-done | bytes 524304 | tf_op jit(solution)/shard_map/reduce_scatter | solution.py:210
  836.5 88.7 %reduce-scatter.16.cloned.1.call-done = bf16[512,512]{1,0:T(8,128)(2,1)} async-done(((bf16[4096,512]{1,0:T(8,128)(2,1)}), bf16[512,512]{1,0:T(8,128)(2,1)}) %reduce-scatter.16.cloned.1.call-update) | async-done | bytes 524304 | tf_op jit(solution)/shard_map/reduce_scatter | solution.py:213
  950.5 14.7 reduce-scatter.20.cloned.1.call-done
  970.5 10.1 all-to-all-done.1
  983.5 19.0 reduce-scatter.18.cloned.1.call-done
  1004.1 121.9 %all-reduce = (f32[]{:T(128)}, f32[1024]{0:T(1024)}, f32[1024]{0:T(1024)}) all-reduce(f32[]{:T(128)} %multiply_reduce_fusion.5, f32[1024]{0:T(1024)S(1)} %get-tuple-element.228, f32[1024]{0:T(1024)S(1)} %copy-done.19), channel_id=1, replica_groups=mesh['shard'=2,'ctx'=8,'tp'=2] {'shard','ctx','tp'}, use_global_device_ids=true, to_apply=%region_10.11 | all-reduce | flops 2049 | bytes 16392 | tf_op jit(solution)/shard_map/psum | solution.py:190
  1129.8 847.7 %all-gather.42.cloned.1.call-done = bf16[4096,6272]{1,0:T(8,128)(2,1)} async-done(((bf16[512,6272]{1,0:T(8,128)(2,1)}), bf16[4096,6272]{1,0:T(8,128)(2,1)}) %all-gather.42.cloned.1.call-update) | async-done | bytes 51380240 | tf_op jit(solution)/shard_map/all_gather | solution.py:12
  1977.5 22.0 %reduce_sum.146 = bf16[512,6272]{1,0:T(8,128)(2,1)} reduce(bf16[8,512,6272]{2,1,0:T(8,128)(2,1)} %bitcast.138, bf16[]{:T(256)} %constant.109.clone.1), dimensions={0}, to_apply=%region_27.28 | reduce | flops 22478848 | bytes 57802752 | tf_op jit(solution)/shard_map/reduce_sum | solution.py:12
  2002.8 8.5 convert_element_type.183
  (329 shorter events, 350.7 us)
Async XLA Ops:
  7.2 42.4 %copy-start.15 = (bf16[1,256,1024]{2,1,0:T(8,128)(2,1)S(1)}, bf16[1,256,1024]{2,1,0:T(8,128)(2,1)}, u32[]{:S(2)}) copy-start(bf16[1,256,1024]{2,1,0:T(8,128)(2,1)} %param.19) | copy-start | bytes 1572868
  7.2 28.7 %all-gather.16.cloned.1.call-start = ((), (), s32[]{:S(2)}) async-start(), calls=%async_computation.9 | async-start | bytes 1572864 | tf_op jit(solution)/shard_map/all_gather | solution.py:159
  11.7 34.8 %all-gather.20.cloned.1.call-start = ((), (), s32[]{:S(2)}) async-start(), calls=%async_computation.11 | async-start | bytes 1572864 | tf_op jit(solution)/shard_map/all_gather | solution.py:147
  12.5 49.0 %all-gather.24.cloned.1.call-start = ((), (), s32[]{:S(2)}) async-start(), calls=%async_computation.13 | async-start | bytes 1572864 | tf_op jit(solution)/shard_map/all_gather | solution.py:148
  13.2 56.7 %all-gather.18.cloned.1.call-start = ((), (), s32[]{:S(2)}) async-start(), calls=%async_computation.10 | async-start | bytes 1572864 | tf_op jit(solution)/shard_map/all_gather | solution.py:146
  13.8 133.3 %all-gather.22.cloned.1.call-start = ((), (), s32[]{:S(2)}) async-start(), calls=%async_computation.12 | async-start | bytes 4718592 | tf_op jit(solution)/shard_map/all_gather | solution.py:174
  49.6 171.7 %all-gather.26.cloned.1.call-start = ((), (), s32[]{:S(2)}) async-start(), calls=%async_computation.14 | async-start | bytes 4718592 | tf_op jit(solution)/shard_map/all_gather | solution.py:175
  64.2 230.2 %all-gather.28.cloned.1.call-start = ((), (), s32[]{:S(2)}) async-start(), calls=%async_computation.15 | async-start | bytes 1572864 | tf_op jit(solution)/shard_map/all_gather | solution.py:151
  65.0 263.2 %reduce-scatter.8.cloned.1.call-start = ((), (), s32[]{:S(2)}) async-start(), calls=%async_computation.16 | async-start | bytes 3145728 | tf_op jit(solution)/shard_map/reduce_scatter | solution.py:162
  294.4 35.2 %copy-start.17 = (f32[1024]{0:T(1024)S(1)}, f32[1024]{0:T(1024)}, u32[]{:S(2)}) copy-start(f32[1024]{0:T(1024)} %param.24) | copy-start | bytes 12292
  297.9 43.6 %all-gather.32.cloned.1.call-start = ((), (), s32[]{:S(2)}) async-start(), calls=%async_computation.18 | async-start | bytes 4325376 | tf_op jit(solution)/shard_map/all_gather | solution.py:149
  298.7 67.4 %all-gather.30.cloned.1.call-start = ((), (), s32[]{:S(2)}) async-start(), calls=%async_computation.17 | async-start | bytes 1572864 | tf_op jit(solution)/shard_map/all_gather | solution.py:159
  330.6 48.9 %all-gather.34.cloned.1.call-start = ((), (), s32[]{:S(2)}) async-start(), calls=%async_computation.19 | async-start | bytes 4325376 | tf_op jit(solution)/shard_map/all_gather | solution.py:150
  331.3 62.6 %all-gather.36.cloned.1.call-start = ((), (), s32[]{:S(2)}) async-start(), calls=%async_computation.20 | async-start | bytes 4325376 | tf_op jit(solution)/shard_map/all_gather | solution.py:152
  331.9 109.7 %reduce-scatter.10.cloned.1.call-start = ((), (), s32[]{:S(2)}) async-start(), calls=%async_computation.21 | async-start | bytes 3145728 | tf_op jit(solution)/shard_map/reduce_scatter | solution.py:162
  393.9 47.7 %copy-start.5 = (bf16[1,256,1024]{2,1,0:T(8,128)(2,1)S(1)}, bf16[1,256,1024]{2,1,0:T(8,128)(2,1)}, u32[]{:S(2)}) copy-start(bf16[1,256,1024]{2,1,0:T(8,128)(2,1)} %param.20) | copy-start | bytes 1572868
  399.4 66.0 %all-gather.38.cloned.1.call-start = ((), (), s32[]{:S(2)}) async-start(), calls=%async_computation.22 | async-start | bytes 1572864 | tf_op jit(solution)/shard_map/all_gather | solution.py:159
  443.9 66.0 %reduce-scatter.12.cloned.1.call-start = ((), (), s32[]{:S(2)}) async-start(), calls=%async_computation.23 | async-start | bytes 3145728 | tf_op jit(solution)/shard_map/reduce_scatter | solution.py:162
  474.7 35.2 %copy-start.4 = (f32[256,1024]{1,0:T(8,128)S(1)}, f32[256,1024]{1,0:T(8,128)}, u32[]{:S(2)}) copy-start(f32[256,1024]{1,0:T(8,128)} %reduce-scatter.10.cloned.1.call-done) | copy-start | bytes 3145732
  477.9 57.6 %all-gather.40.cloned.1.call-start = ((), (), s32[]{:S(2)}) async-start(), calls=%async_computation.24 | async-start | bytes 1572864 | tf_op jit(solution)/shard_map/all_gather | solution.py:159
  514.0 319.8 %reduce-scatter.14.cloned.1.call-start = ((), (), s32[]{:S(2)}) async-start(), calls=%async_computation.25 | async-start | bytes 4718592 | tf_op jit(solution)/shard_map/reduce_scatter | solution.py:210
  745.2 179.9 %reduce-scatter.16.cloned.1.call-start = ((), (), s32[]{:S(2)}) async-start(), calls=%async_computation.26 | async-start | bytes 4718592 | tf_op jit(solution)/shard_map/reduce_scatter | solution.py:213
  751.9 213.3 %reduce-scatter.20.cloned.1.call-start = ((), (), s32[]{:S(2)}) async-start(), calls=%async_computation.28 | async-start | bytes 19267584 | tf_op jit(solution)/shard_map/reduce_scatter | solution.py:234
  943.5 59.0 %reduce-scatter.18.cloned.1.call-start = ((), (), s32[]{:S(2)}) async-start(), calls=%async_computation.27 | async-start | bytes 3145728 | tf_op jit(solution)/shard_map/reduce_scatter | solution.py:162
  950.4 1027.1 %all-gather.42.cloned.1.call-start = ((), (), s32[]{:S(2)}) async-start(), calls=%async_computation.29 | async-start | bytes 57802752 | tf_op jit(solution)/shard_map/all_gather | solution.py:12
  965.2 37.3 %copy-start.3 = (bf16[1,256,1024]{2,1,0:T(8,128)(2,1)S(1)}, bf16[1,256,1024]{2,1,0:T(8,128)(2,1)}, u32[]{:S(2)}) copy-start(bf16[1,256,1024]{2,1,0:T(8,128)(2,1)} %param.18) | copy-start | bytes 1572868
  965.2 37.3 %copy-start.18 = (f32[1024]{0:T(1024)S(1)}, f32[1024]{0:T(1024)}, u32[]{:S(2)}) copy-start(f32[1024]{0:T(1024)} %param.23) | copy-start | bytes 12292
  965.2 37.3 %copy-start.21 = (f32[256]{0:T(256)S(1)}, f32[256]{0:T(256)}, u32[]{:S(2)}) copy-start(f32[256]{0:T(256)} %copy-done.20) | copy-start | bytes 3076
  966.1 38.0 %copy-start.19 = (f32[1024]{0:T(1024)S(1)}, f32[1024]{0:T(1024)}, u32[]{:S(2)}) copy-start(f32[1024]{0:T(1024)} %get-tuple-element.226) | copy-start | bytes 12292
  966.1 161.2 %copy-start.23 = (f32[256]{0:T(256)S(1)}, f32[256]{0:T(256)}, u32[]{:S(2)}) copy-start(f32[256]{0:T(256)} %copy-done.22) | copy-start | bytes 3076
  966.1 161.2 %copy-start.6 = (f32[256,1024]{1,0:T(8,128)S(1)}, f32[256,1024]{1,0:T(8,128)}, u32[]{:S(2)}) copy-start(f32[256,1024]{1,0:T(8,128)} %get-tuple-element.277) | copy-start | bytes 3145732
  966.1 14.5 all-to-all-start.1
  (44 other events, 310.4 us)
Sparse Core Ops, SparseCore 0:
  11.8 23.9 all-gather.15
  37.4 9.0 all-gather.19
  48.0 10.1 all-gather.23
  59.7 10.1 all-gather.17
  72.5 74.5 all-gather.21
  149.6 71.6 all-gather.25
  222.8 7.2 all-gather.27
  298.1 30.0 reduce-scatter.7
  329.8 11.7 all-gather.31
  343.6 22.4 all-gather.29
  367.7 11.7 all-gather.33
  381.0 12.8 all-gather.35
  399.5 33.4 reduce-scatter.9
  444.0 21.2 all-gather.37
  478.0 31.8 reduce-scatter.11
  514.2 21.2 all-gather.39
  745.3 88.4 reduce-scatter.13
  837.3 87.7 reduce-scatter.15
  943.6 21.5 reduce-scatter.19
  967.9 34.5 reduce-scatter.17
  1004.0 973.4 all-gather.41
